TPU v7x, 32 devices: a whole 2x2x4 slice. The times are simulated.
32 devices in a mesh: strip: 8 (over z, y), chan: 4 (over x, core).
Axes of the slice: x: 2, y: 2, z: 4, core: 2. Of those that a mesh axis runs over, the one named last changes fastest.
Arguments:
- activations: bfloat16 [64, 128, 1280], P('strip', None, 'chan'), may hold values from -17 to 17
- weight: bfloat16 [9, 1280, 1280], P(None, None, 'chan'), may hold values from -0.0546875 to 0.0546875
- gamma: float32 [1280], replicated, may hold values from 0.25 to 1.75
- beta: float32 [1280], replicated, may hold values from -3 to 3
- group_map: int32 [1280], replicated, may hold values from 0 to 31, as said below
- lengths: int32 [8], P('strip'), may hold values from 1 to 8, 48 in all
- stale_edges: bfloat16 [16, 128, 1280], P('strip', None, 'chan'), may hold values from -6 to 6
- stale_mean: float32 [32], replicated, may hold values from -0.5 to 0.5
- stale_square: float32 [32], replicated, may hold values from 1 to 4
- old_mean: float32 [8, 32], P('strip'), may hold values from -0.5 to 0.5
- old_square: float32 [8, 32], P('strip'), may hold values from 0.5 to 6
Outputs:
- upsampled: bfloat16 [128, 256, 1280], P('strip', None, 'chan')
- new_mean: float32 [32], replicated
- new_square: float32 [32], replicated
Inputs may be any that keep to these rules, and one draw needn't show every extreme that they name: `group_map`: every group has exactly 40 channels. The lengths sum to 48, and some strip uses all 8 rows.
All inputs are finite; a program needn't handle non-finite values. No bound on the sum of `lengths` on one device may be relied on, other than what follows from the above.
Results may differ from a plain program's by a relative error of at most 0.0027.
Values may be sent and summed in bfloat16 or wider, within the bound.
A program may use at most 64 MiB of HBM per device.

v0:
```python
import jax
import jax.numpy as jnp
from jax import lax
from jax.sharding import PartitionSpec as P

EPS = 1e-05


def padded_2(block, sides, width):
    for axis, dim in sides:
        count = lax.axis_size(axis)
        forward = [(i, i + 1) for i in range(count - 1)]
        backward = [(target, source) for source, target in forward]
        low = lax.ppermute(
            lax.slice_in_dim(block, block.shape[dim] - width, None, axis=dim), axis, forward
        )
        high = lax.ppermute(lax.slice_in_dim(block, 0, width, axis=dim), axis, backward)
        block = jnp.concatenate([low, block, high], axis=dim)
    return block


def per_device(
    activations,
    weight,
    gamma,
    beta,
    group_map,
    lengths,
    stale_edges,
    stale_mean,
    stale_square,
    old_mean,
    old_square,
):
    rows, width, local_c = activations.shape
    channels = weight.shape[1]
    groups = stale_mean.shape[0]
    per_group = channels // groups
    offset = lax.axis_index("chan") * local_c
    member = (group_map[:, None] == jnp.arange(groups, dtype=jnp.int32)[None, :]).astype(
        jnp.float32
    )
    local_member = lax.dynamic_slice_in_dim(member, offset, local_c, 0)
    length = lengths[0]
    used = (jnp.arange(rows, dtype=jnp.int32) < length).astype(jnp.float32)[:, None, None]
    values = activations.astype(jnp.float32) * used
    chan_sum = jnp.sum(values, axis=(0, 1))
    chan_sq = jnp.sum(values * values, axis=(0, 1))
    part_one = jnp.sum(chan_sum[:, None] * local_member, axis=0)
    part_two = jnp.sum(chan_sq[:, None] * local_member, axis=0)
    strip_one, strip_two = lax.psum((part_one, part_two), "chan")
    total_count = float(lax.axis_size("strip") * (3 * rows // 4) * width * per_group)
    image_one, image_two = lax.psum((strip_one, strip_two), "strip")
    new_mean = image_one / total_count
    new_square = image_two / total_count
    count = length.astype(jnp.float32) * (width * per_group)
    fresh_mean = strip_one / count
    fresh_square = strip_two / count
    mean_g = stale_mean + fresh_mean - old_mean[0]
    square_g = stale_square + fresh_square - old_square[0]
    var_g = jnp.maximum(square_g - mean_g * mean_g, 0.5 * (fresh_square - fresh_mean * fresh_mean))
    rstd_g = lax.rsqrt(var_g + EPS)
    scale_c = jnp.sum(member * rstd_g[None, :], axis=1) * gamma
    shift_c = beta - jnp.sum(member * mean_g[None, :], axis=1) * scale_c
    bordered = padded_2(stale_edges, (("strip", 0),), 1)
    bounds = jnp.stack([bordered[0], bordered[3]], axis=0)
    initial = jnp.zeros((rows * width, local_c), jnp.float32)
    total = initial
    piece = lax.all_gather(activations, "chan", axis=2, tiled=True)
    bound = lax.all_gather(bounds, "chan", axis=2, tiled=True)
    depth = piece.shape[2]
    act = (jax.nn.silu(piece.astype(jnp.float32) * scale_c + shift_c) * used).astype(jnp.bfloat16)
    padded = jnp.concatenate([bound[0:1], act, jnp.zeros((1, width, depth), jnp.bfloat16)], axis=0)
    place = (jnp.arange(rows + 2, dtype=jnp.int32) == length + 1)[:, None, None]
    padded = jnp.where(place, bound[1][None], padded)
    padded = jnp.pad(padded, ((0, 0), (1, 1), (0, 0)))
    for tap in range(9):
        down, across = (tap // 3, tap % 3)
        patch = padded[down : down + rows, across : across + width].reshape(rows * width, depth)
        total = total + jnp.dot(patch, weight[tap], preferred_element_type=jnp.float32)
    block = ((activations.astype(jnp.float32) + total.reshape(rows, width, local_c)) * used).astype(
        jnp.bfloat16
    )
    upsampled = jnp.repeat(jnp.repeat(block, 2, axis=0), 2, axis=1)
    return (upsampled, new_mean, new_square)


def solution(mesh):
    in_specs = (
        P("strip", None, "chan"),
        P(None, None, "chan"),
        P(),
        P(),
        P(),
        P("strip"),
        P("strip", None, "chan"),
        P(),
        P(),
        P("strip", None),
        P("strip", None),
    )
    out_specs = (P("strip", None, "chan"), P(), P())
    return jax.shard_map(
        per_device, mesh=mesh, in_specs=in_specs, out_specs=out_specs, check_vma=False
    )
```

profile of v0, /device:TPU:0, one launch (start us, length us, event | category | flops | bytes accessed | tf_op | source)
XLA Modules:
  0.0 100.3 jit_solution(1135148588902950023)
XLA Ops:
  7.3 2.4 %copy.49 = bf16[8,128,320]{1,0,2:T(8,128)(2,1)} copy(bf16[8,128,320]{1,2,0:T(8,128)(2,1)} %param.11) | data formatting | bytes 1310720 | tf_op args[0]
  9.7 0.9 fusion.30
  10.8 1.3 %collective-permute-start.1 = (bf16[1,128,320]{1,0,2:T(2,128)(2,1)S(1)}, bf16[1,128,320]{1,0,2:T(2,128)(2,1)S(1)}, u32[]{:S(2)}, u32[]{:S(2)}) collective-permute-start(bf16[1,128,320]{1,0,2:T(2,128)(2,1)S(1)} %copy.55), channel_id=1, source_target_pairs={{4,0},{8,4},{12,8},{16,12},{20,16},{24,20},{28,24},{5,1},{9,5},{13... | collective-permute-start | bytes 245768 | tf_op jit(solution)/shard_map/ppermute | solution.py:17
  12.2 5.5 %collective-permute-start = (bf16[1,128,320]{1,0,2:T(2,128)(2,1)S(1)}, bf16[1,128,320]{1,0,2:T(2,128)(2,1)S(1)}, u32[]{:S(2)}, u32[]{:S(2)}) collective-permute-start(bf16[1,128,320]{1,0,2:T(2,128)(2,1)S(1)} %copy.54), channel_id=1, source_target_pairs={{0,4},{4,8},{8,12},{12,16},{16,20},{20,24},{24,28},{1,5},{5,9},{9,... | collective-permute-start | bytes 245768 | tf_op jit(solution)/shard_map/ppermute | solution.py:14
  19.1 7.3 %all-reduce.2 = (f32[32]{0:T(128)S(1)}, f32[32]{0:T(128)S(1)}) all-reduce(f32[32]{0:T(128)S(1)} %get-tuple-element.21, f32[32]{0:T(128)S(1)} %get-tuple-element.20), channel_id=1, replica_groups=mesh['strip'=8,'chan'=4] {'chan'}, use_global_device_ids=true, to_apply=%region_5.0 | all-reduce | flops 64 | bytes 512 | tf_op jit(solution)/shard_map/psum | solution.py:51
  26.5 19.8 %all-reduce.1 = (f32[32]{0:T(128)S(1)}, f32[32]{0:T(128)S(1)}) all-reduce(f32[32]{0:T(128)S(1)} %get-tuple-element.26, f32[32]{0:T(128)S(1)} %get-tuple-element.27), channel_id=1, replica_groups=mesh['strip'=8,'chan'=4] {'strip'}, use_global_device_ids=true, to_apply=%region_8.0 | all-reduce | flops 64 | bytes 512 | tf_op jit(solution)/shard_map/psum | solution.py:53
  47.3 7.5 %all_gather.6 = bf16[2,128,1280]{1,0,2:T(2,128)(2,1)S(1)} all-gather(bf16[2,128,320]{1,0,2:T(2,128)(2,1)S(1)} %pad_maximum_fusion), channel_id=1, replica_groups=mesh['strip'=8,'chan'=4] {'chan'}, dimensions={2}, use_global_device_ids=true | all-gather | bytes 819200 | tf_op jit(solution)/shard_map/all_gather | solution.py:70
  55.8 1.1 %copy.56 = bf16[1,128,1280]{2,1,0:T(8,128)(2,1)} copy(bf16[1,128,1280]{1,0,2:T(2,128)(2,1)S(1)} %get-tuple-element.41) | data formatting | bytes 655360
  56.9 1.1 %copy.57 = bf16[1,128,1280]{2,1,0:T(8,128)(2,1)} copy(bf16[1,128,1280]{1,0,2:T(2,128)(2,1)S(1)} %get-tuple-element.42) | data formatting | bytes 655360
  58.0 3.8 %copy.50 = bf16[8,128,1280]{2,1,0:T(8,128)(2,1)S(1)} copy(bf16[8,128,1280]{1,0,2:T(8,128)(2,1)} %all-gather.2.cloned.1.call-done) | data formatting | bytes 5242880 | tf_op jit(solution)/shard_map/all_gather | solution.py:69
  61.9 1.7 %multiply_convert_fusion = bf16[8,128,1280]{2,1,0:T(8,128)(2,1)S(1)} fusion(bf16[8,128,1280]{2,1,0:T(8,128)(2,1)S(1)} %copy.50, f32[8]{0:T(128)S(1)} %compare_convert_fusion, f32[1280]{0:T(1024)S(1)} %get-tuple-element.28, f32[1280]{0:T(1024)S(1)} %get-tuple-element.29), kind=kLoop, calls=%fused_computation | loop fusion | flops 11796480 | bytes 5253152 | tf_op jit(solution)/shard_map/convert_element_type | solution.py:72
  64.0 10.0 %pad_slice_fusion = (bf16[8,128,1280]{2,1,0:T(8,128)(2,1)S(1)}, bf16[8,128,1280]{2,1,0:T(8,128)(2,1)S(1)}, bf16[8,128,1280]{2,1,0:T(8,128)(2,1)S(1)}, bf16[8,128...) fusion(bf16[10,128,1280]{2,1,0:T(8,128)(2,1)S(1)} %maximum_sele, ...), kind=kLoop, calls=%fused_computation.2 | loop fusion | bytes 34734080 | tf_op jit(solution)/shard_map/slice | solution.py:79
  74.1 2.3 %fusion.14 = f32[1024,320]{0,1:T(8,128)S(1)} fusion(bf16[1024,1280]{1,0:T(8,128)(2,1)S(1)} %bitcast.78, bf16[9,1280,320]{1,2,0:T(8,128)(2,1)} %param.12), kind=kOutput, calls=%fused_computation.32 | convolution fusion | flops 838860800 | bytes 4751360 | tf_op jit(solution)/shard_map/dot_general | solution.py:80
  76.4 2.3 %convolution_add_fusion.7 = f32[1024,320]{0,1:T(8,128)S(1)} fusion(f32[1024,320]{0,1:T(8,128)S(1)} %fusion.14, bf16[1024,1280]{1,0:T(8,128)(2,1)S(1)} %bitcast.77, bf16[9,1280,320]{1,2,0:T(8,128)(2,1)} %param.12), kind=kOutput, calls=%fused_computation.20 | convolution fusion | flops 839188480 | bytes 6062080 | tf_op jit(solution)/shard_map/dot_general | solution.py:80
  78.8 1.1 %convolution_add_fusion.6 = f32[1024,320]{0,1:T(8,128)S(1)} fusion(f32[1024,320]{0,1:T(8,128)S(1)} %convolution_add_fusion.7, bf16[1024,1280]{1,0:T(8,128)(2,1)S(1)} %bitcast.76, bf16[9,1280,320]{1,2,0:T(8,128)(2,1)S(1)} %bitcast.81), kind=kOutput, calls=%fused_computation.19 | convolution fusion | flops 839188480 | bytes 6062080 | tf_op jit(solution)/shard_map/dot_general | solution.py:80
  79.9 1.0 %convolution_add_fusion.5 = f32[1024,320]{0,1:T(8,128)S(1)} fusion(f32[1024,320]{0,1:T(8,128)S(1)} %convolution_add_fusion.6, bf16[1024,1280]{1,0:T(8,128)(2,1)S(1)} %bitcast.75, bf16[9,1280,320]{1,2,0:T(8,128)(2,1)S(1)} %bitcast.81), kind=kOutput, calls=%fused_computation.18 | convolution fusion | flops 839188480 | bytes 6062080 | tf_op jit(solution)/shard_map/dot_general | solution.py:80
  80.9 1.1 %convolution_add_fusion.4 = f32[1024,320]{0,1:T(8,128)S(1)} fusion(f32[1024,320]{0,1:T(8,128)S(1)} %convolution_add_fusion.5, bf16[1024,1280]{1,0:T(8,128)(2,1)S(1)} %bitcast.74, bf16[9,1280,320]{1,2,0:T(8,128)(2,1)S(1)} %bitcast.81), kind=kOutput, calls=%fused_computation.17 | convolution fusion | flops 839188480 | bytes 6062080 | tf_op jit(solution)/shard_map/dot_general | solution.py:80
  82.0 1.1 %convolution_add_fusion.3 = f32[1024,320]{0,1:T(8,128)S(1)} fusion(f32[1024,320]{0,1:T(8,128)S(1)} %convolution_add_fusion.4, bf16[1024,1280]{1,0:T(8,128)(2,1)S(1)} %bitcast.73, bf16[9,1280,320]{1,2,0:T(8,128)(2,1)S(1)} %bitcast.81), kind=kOutput, calls=%fused_computation.16 | convolution fusion | flops 839188480 | bytes 6062080 | tf_op jit(solution)/shard_map/dot_general | solution.py:80
  83.0 1.1 %convolution_add_fusion.2 = f32[1024,320]{0,1:T(8,128)S(1)} fusion(f32[1024,320]{0,1:T(8,128)S(1)} %convolution_add_fusion.3, bf16[1024,1280]{1,0:T(8,128)(2,1)S(1)} %bitcast.72, bf16[9,1280,320]{1,2,0:T(8,128)(2,1)S(1)} %bitcast.81), kind=kOutput, calls=%fused_computation.15 | convolution fusion | flops 839188480 | bytes 6062080 | tf_op jit(solution)/shard_map/dot_general | solution.py:80
  84.1 1.1 %convolution_add_fusion.1 = f32[1024,320]{0,1:T(8,128)S(1)} fusion(f32[1024,320]{0,1:T(8,128)S(1)} %convolution_add_fusion.2, bf16[1024,1280]{1,0:T(8,128)(2,1)S(1)} %bitcast.71, bf16[9,1280,320]{1,2,0:T(8,128)(2,1)S(1)} %bitcast.81), kind=kOutput, calls=%fused_computation.14 | convolution fusion | flops 839188480 | bytes 6062080 | tf_op jit(solution)/shard_map/dot_general | solution.py:80
  85.2 1.1 %fusion.2 = f32[40,8,8,128]{3,2,1,0:T(8,128)S(1)} fusion(f32[1024,320]{0,1:T(8,128)S(1)} %convolution_add_fusion.1, bf16[1024,1280]{1,0:T(8,128)(2,1)S(1)} %bitcast.70, bf16[9,1280,320]{1,2,0:T(8,128)(2,1)S(1)} %bitcast.81), kind=kOutput, calls=%fused_computation.13 | convolution fusion | flops 839188480 | bytes 6062080 | tf_op jit(solution)/shard_map/dot_general | solution.py:80
  86.7 1.9 %copy.52 = bf16[16,128,320]{2,0,1:T(8,128)(2,1)} copy(bf16[16,128,320]{1,2,0:T(8,128)(2,1)S(1)} %bitcast.69) | data formatting | bytes 2621440 | tf_op jit(solution)/shard_map/reshape | solution.py:84
  88.6 1.7 %broadcast_in_dim.42 = bf16[16,128,2,320]{3,0,2,1:T(8,128)(2,1)S(1)} broadcast(bf16[16,128,320]{2,0,1:T(8,128)(2,1)} %copy.52), dimensions={0,1,3} | broadcast | bytes 3932160 | tf_op jit(solution)/shard_map/broadcast_in_dim | solution.py:84
  90.3 3.1 %copy.53 = bf16[16,256,320]{1,2,0:T(8,128)(2,1)} copy(bf16[16,256,320]{2,0,1:T(8,128)(2,1)S(1)} %bitcast.68) | data formatting | bytes 5242880
  (47 shorter events, 4.0 us)
Async XLA Ops:
  7.2 11.4 %copy-start = (bf16[8,128,320]{1,2,0:T(8,128)(2,1)S(1)}, bf16[8,128,320]{1,2,0:T(8,128)(2,1)}, u32[]{:S(2)}) copy-start(bf16[8,128,320]{1,2,0:T(8,128)(2,1)} %param.11) | copy-start | bytes 1966084
  7.2 11.7 %copy-start.3 = (s32[1280]{0:T(1024)S(1)}, s32[1280]{0:T(1024)}, u32[]{:S(2)}) copy-start(s32[1280]{0:T(1024)} %param.15) | copy-start | bytes 15364
  7.2 39.0 %copy-start.6 = (f32[1,32]{1,0:T(1,128)S(1)}, f32[1,32]{1,0:T(1,128)}, u32[]{:S(2)}) copy-start(f32[1,32]{1,0:T(1,128)} %param.21) | copy-start | bytes 388
  7.2 39.0 %copy-start.8 = (f32[1,32]{1,0:T(1,128)S(1)}, f32[1,32]{1,0:T(1,128)}, u32[]{:S(2)}) copy-start(f32[1,32]{1,0:T(1,128)} %param.20) | copy-start | bytes 388
  7.2 39.0 %copy-start.7 = (f32[32]{0:T(128)S(1)}, f32[32]{0:T(128)}, u32[]{:S(2)}) copy-start(f32[32]{0:T(128)} %param.19) | copy-start | bytes 388
  7.2 39.0 %copy-start.9 = (f32[32]{0:T(128)S(1)}, f32[32]{0:T(128)}, u32[]{:S(2)}) copy-start(f32[32]{0:T(128)} %param.18) | copy-start | bytes 388
  7.2 39.7 %copy-start.4 = (f32[1280]{0:T(1024)S(1)}, f32[1280]{0:T(1024)}, u32[]{:S(2)}) copy-start(f32[1280]{0:T(1024)} %param.14) | copy-start | bytes 15364
  7.2 39.7 %copy-start.5 = (f32[1280]{0:T(1024)S(1)}, f32[1280]{0:T(1024)}, u32[]{:S(2)}) copy-start(f32[1280]{0:T(1024)} %param.13) | copy-start | bytes 15364
  7.2 50.8 %all-gather.2.cloned.1.call-start = ((), (), s32[]{:S(2)}) async-start(), calls=%async_computation | async-start | bytes 3276800 | tf_op jit(solution)/shard_map/all_gather | solution.py:69
  10.8 36.1 %collective-permute-start.1 = (bf16[1,128,320]{1,0,2:T(2,128)(2,1)S(1)}, bf16[1,128,320]{1,0,2:T(2,128)(2,1)S(1)}, u32[]{:S(2)}, u32[]{:S(2)}) collective-permute-start(bf16[1,128,320]{1,0,2:T(2,128)(2,1)S(1)} %copy.55), channel_id=1, source_target_pairs={{4,0},{8,4},{12,8},{16,12},{20,16},{24,20},{28,24},{5,1},{9,5},{13... | collective-permute-start | bytes 245768 | tf_op jit(solution)/shard_map/ppermute | solution.py:17
  12.2 34.7 %collective-permute-start = (bf16[1,128,320]{1,0,2:T(2,128)(2,1)S(1)}, bf16[1,128,320]{1,0,2:T(2,128)(2,1)S(1)}, u32[]{:S(2)}, u32[]{:S(2)}) collective-permute-start(bf16[1,128,320]{1,0,2:T(2,128)(2,1)S(1)} %copy.54), channel_id=1, source_target_pairs={{0,4},{4,8},{8,12},{12,16},{16,20},{20,24},{24,28},{1,5},{5,9},{9,... | collective-permute-start | bytes 245768 | tf_op jit(solution)/shard_map/ppermute | solution.py:14
  61.8 1.7 %copy-start.1 = (bf16[1,128,1280]{2,1,0:T(8,128)(2,1)S(1)}, bf16[1,128,1280]{2,1,0:T(8,128)(2,1)}, u32[]{:S(2)}) copy-start(bf16[1,128,1280]{2,1,0:T(8,128)(2,1)} %copy.56) | copy-start | bytes 983044
  61.9 1.7 %copy-start.2 = (bf16[1,128,1280]{2,1,0:T(8,128)(2,1)S(1)}, bf16[1,128,1280]{2,1,0:T(8,128)(2,1)}, u32[]{:S(2)}) copy-start(bf16[1,128,1280]{2,1,0:T(8,128)(2,1)} %copy.57) | copy-start | bytes 983044
  74.1 4.7 %slice-start = ((s8[7372800]{0:T(1024)(128)(4,1)}), s8[4194304]{0:T(1024)(128)(4,1)S(1)}, s32[]{:S(2)}) async-start(s8[7372800]{0:T(1024)(128)(4,1)} %bitcast.80), calls=%async_computation.1 | async-start | bytes 8388608
  76.4 2.4 %slice-start.1 = ((s8[7372800]{0:T(1024)(128)(4,1)}), s8[3178496]{0:T(1024)(128)(4,1)S(1)}, s32[]{:S(2)}) async-start(s8[7372800]{0:T(1024)(128)(4,1)} %bitcast.80), calls=%async_computation.2 | async-start | bytes 6356992
Sparse Core Ops, SparseCore 0:
  10.2 28.4 all-gather.1
where the time goes:
time: 101 us; the launch traced here: 100 us
  blocking collectives  34.6 us (34%)
  local copies, waits for them, and re-layouts  27.7 us (27%)
  between operations  15.1 us (15%)
  matrix products  12 us (12%)
  starting transfers between devices  6.87 us (7%)
  other arithmetic  3.98 us (4%)
    psum x1, blocking collectives, per_device(): image_one, image_two = lax.psum((strip_one, strip_two), 'strip')  19.8 us
    dot_general x9, matrix products, per_device(): jnp.dot(patch, weight[tap], preferred_element_type=jnp.float32)  12 us
    slice x1, local copies, waits for them, and re-layouts, per_device(): padded[down:down + rows, across:across + width].reshape(rows * width, depth)  10 us
    unnamed x30, local copies, waits for them, and re-layouts  8.07 us
    all_gather x1, blocking collectives, per_device(): bound = lax.all_gather(bounds, 'chan', axis=2, tiled=True)  7.51 us
    psum x1, blocking collectives, per_device(): strip_one, strip_two = lax.psum((part_one, part_two), 'chan')  7.31 us
    ppermute x1, starting transfers between devices, padded_2(): lax.ppermute(lax.slice_in_dim(block, block.shape[dim] - width, None, axis...  5.54 us
    all_gather x1, local copies, waits for them, and re-layouts, per_device(): piece = lax.all_gather(activations, 'chan', axis=2, tiled=True)  3.82 us
  transfers between devices with their start and end apart: 3, of which 0 were waited for; matrix products, arithmetic and copies ran while one was open for 6% of the time, Pallas kernels for 0%

commit v1 on v0

--- a/solution.py
+++ b/solution.py
@@ -4,6 +4,17 @@
 from jax.sharding import PartitionSpec as P
 
 EPS = 1e-05
+
+
+def pass_along(x, axis, dim):
+    size = lax.axis_size(axis)
+    right = [(i, (i + 1) % size) for i in range(size)]
+    terms = [x]
+    for stride in range(1, size):
+        terms = [lax.ppermute(terms[0], axis, right), *terms]
+    whole = jnp.concatenate(terms, axis=dim)
+    turn = (lax.axis_index(axis) + 1) * terms[-1].shape[dim]
+    return jnp.roll(whole, turn, axis=dim)
 
 
 def padded_2(block, sides, width):
@@ -67,7 +78,7 @@
     initial = jnp.zeros((rows * width, local_c), jnp.float32)
     total = initial
     piece = lax.all_gather(activations, "chan", axis=2, tiled=True)
-    bound = lax.all_gather(bounds, "chan", axis=2, tiled=True)
+    bound = pass_along(bounds, "chan", 2)
     depth = piece.shape[2]
     act = (jax.nn.silu(piece.astype(jnp.float32) * scale_c + shift_c) * used).astype(jnp.bfloat16)
     padded = jnp.concatenate([bound[0:1], act, jnp.zeros((1, width, depth), jnp.bfloat16)], axis=0)

time: 101 us -> 105 us (1.040)
  waiting for transfers between devices: 0.02 us -> 9.57 us
  blocking collectives: 34.6 us -> 29.6 us
    ppermute x0 -> x3, waiting for transfers between devices: none -> 9.54 us  [pass_along(): terms = [lax.ppermute(terms[0], axis, right), *terms]]
    all_gather x1 -> x0, blocking collectives: 7.51 us -> none  [per_device(): bound = lax.all_gather(bounds, 'chan', axis=2, tiled=True)]
    psum x1, blocking collectives: 19.8 us -> 22.6 us  [per_device(): image_one, image_two = lax.psum((strip_one, strip_two), 'strip')]
    concatenate x0 -> x1, local copies, waits for them, and re-layouts: none -> 2.38 us  [pass_along(): return jnp.roll(whole, turn, axis=dim)]
    unnamed x30 -> x29, local copies, waits for them, and re-layouts: 8.07 us -> 5.86 us
    broadcast_in_dim x0 -> x1, local copies, waits for them, and re-layouts: none -> 1.12 us  [per_device(): padded = jnp.where(place, bound[1][None], padded)]
  transfers between devices with their start and end apart: 3 -> 6, of which waited for: 0 -> 2; matrix products, arithmetic and copies ran while one was open for 6% -> 6% of each run, Pallas kernels for 0% -> 0%
where the time goes in v1:
time: 105 us; the launch traced here: 104 us
  blocking collectives  29.6 us (28%)
  local copies, waits for them, and re-layouts  28.1 us (27%)
  between operations  15.1 us (14%)
  matrix products  12 us (11%)
  waiting for transfers between devices  9.57 us (9%)
  starting transfers between devices  6.35 us (6%)
  other arithmetic  3.6 us (3%)
    psum x1, blocking collectives, per_device(): image_one, image_two = lax.psum((strip_one, strip_two), 'strip')  22.6 us
    dot_general x9, matrix products, per_device(): jnp.dot(patch, weight[tap], preferred_element_type=jnp.float32)  12 us
    slice x1, local copies, waits for them, and re-layouts, per_device(): padded[down:down + rows, across:across + width].reshape(rows * width, depth)  10 us
    ppermute x3, waiting for transfers between devices, pass_along(): terms = [lax.ppermute(terms[0], axis, right), *terms]  9.54 us
    psum x1, blocking collectives, per_device(): strip_one, strip_two = lax.psum((part_one, part_two), 'chan')  6.92 us
    unnamed x29, local copies, waits for them, and re-layouts  5.86 us
    ppermute x1, starting transfers between devices, padded_2(): lax.ppermute(lax.slice_in_dim(block, block.shape[dim] - width, None, axis...  4.9 us
    all_gather x1, local copies, waits for them, and re-layouts, per_device(): piece = lax.all_gather(activations, 'chan', axis=2, tiled=True)  3.82 us
  transfers between devices with their start and end apart: 6, of which 2 were waited for; matrix products, arithmetic and copies ran while one was open for 6% of the time, Pallas kernels for 0%

profile of v1, /device:TPU:0, one launch (start us, length us, event | category | flops | bytes accessed | tf_op | source)
XLA Modules:
  0.0 104.3 jit_solution(7957578673530825882)
XLA Ops:
  7.3 2.4 %copy.36 = bf16[8,128,320]{1,0,2:T(8,128)(2,1)} copy(bf16[8,128,320]{1,2,0:T(8,128)(2,1)} %param.11) | data formatting | bytes 1310720 | tf_op args[0]
  10.8 4.9 %collective-permute-start = (bf16[1,128,320]{2,1,0:T(8,128)(2,1)S(1)}, bf16[1,128,320]{2,1,0:T(8,128)(2,1)S(1)}, u32[]{:S(2)}, u32[]{:S(2)}) collective-permute-start(bf16[1,128,320]{2,1,0:T(8,128)(2,1)S(1)} %copy.41), channel_id=1, source_target_pairs={{0,4},{4,8},{8,12},{12,16},{16,20},{20,24},{24,28},{1,5},{5,9},{9,... | collective-permute-start | bytes 245768 | tf_op jit(solution)/shard_map/ppermute | solution.py:25
  15.8 1.3 %collective-permute-start.1 = (bf16[1,128,320]{2,1,0:T(8,128)(2,1)S(1)}, bf16[1,128,320]{2,1,0:T(8,128)(2,1)S(1)}, u32[]{:S(2)}, u32[]{:S(2)}) collective-permute-start(bf16[1,128,320]{2,1,0:T(8,128)(2,1)S(1)} %copy.42), channel_id=1, source_target_pairs={{4,0},{8,4},{12,8},{16,12},{20,16},{24,20},{28,24},{5,1},{9,5},{13... | collective-permute-start | bytes 245768 | tf_op jit(solution)/shard_map/ppermute | solution.py:28
  18.4 6.9 %all-reduce.2 = (f32[32]{0:T(128)S(1)}, f32[32]{0:T(128)S(1)}) all-reduce(f32[32]{0:T(128)S(1)} %get-tuple-element.18, f32[32]{0:T(128)S(1)} %get-tuple-element.17), channel_id=1, replica_groups=mesh['strip'=8,'chan'=4] {'chan'}, use_global_device_ids=true, to_apply=%region_5.0 | all-reduce | flops 64 | bytes 512 | tf_op jit(solution)/shard_map/psum | solution.py:62
  25.5 22.6 %all-reduce.1 = (f32[32]{0:T(128)S(1)}, f32[32]{0:T(128)S(1)}) all-reduce(f32[32]{0:T(128)S(1)} %get-tuple-element.23, f32[32]{0:T(128)S(1)} %get-tuple-element.24), channel_id=1, replica_groups=mesh['strip'=8,'chan'=4] {'strip'}, use_global_device_ids=true, to_apply=%region_8.0 | all-reduce | flops 64 | bytes 512 | tf_op jit(solution)/shard_map/psum | solution.py:64
  48.4 5.0 %collective-permute-done.3 = bf16[2,128,320]{2,1,0:T(8,128)(2,1)S(1)} collective-permute-done((bf16[2,128,320]{2,1,0:T(8,128)(2,1)S(1)}, bf16[2,128,320]{2,1,0:T(8,128)(2,1)S(1)}, u32[]{:S(2)}, u32[]{:S(2)}) %collective-permute-start.3) | collective-permute-done | bytes 163872 | tf_op jit(solution)/shard_map/ppermute | solution.py:14
  54.1 4.5 %collective-permute-done.4 = bf16[2,128,320]{2,1,0:T(8,128)(2,1)S(1)} collective-permute-done((bf16[2,128,320]{2,1,0:T(8,128)(2,1)S(1)}, bf16[2,128,320]{2,1,0:T(8,128)(2,1)S(1)}, u32[]{:S(2)}, u32[]{:S(2)}) %collective-permute-start.4) | collective-permute-done | bytes 163872 | tf_op jit(solution)/shard_map/ppermute | solution.py:14
  58.6 2.4 %concatenate.9 = bf16[2,128,2560]{2,1,0:T(8,128)(2,1)S(1)} concatenate(bf16[2,128,320]{2,1,0:T(8,128)(2,1)S(1)} %collective-permute-done.4, bf16[2,128,320]{2,1,0:T(8,128)(2,1)S(1)} %collective-permute-done.3, bf16[2,128,320]{2,1,0:T(8,128)(2,1)S(1)} %collective-permute-done.2, bf16[2,128,320]{2,1,0:T(8,128)(2,1)S(1)} %constant_dynamic-update-slice_fusion, ...), dimensions={2} | concatenate | bytes 2621440 | tf_op jit(solution)/shard_map/jit(_roll_dynamic)/concatenate | solution.py:17
  60.9 1.1 %dynamic-slice_bitcast_fusion = (bf16[128,1280]{1,0:T(8,128)(2,1)}, bf16[1,128,1280]{2,1,0:T(8,128)(2,1)}) fusion(bf16[2,128,2560]{2,1,0:T(8,128)(2,1)S(1)} %concatenate.9, s32[]{:T(128)S(6)} %add.101, s32[]{:T(128)S(6)} %select_n.21), kind=kLoop, calls=%fused_computation.43 | loop fusion | bytes 1310728 | tf_op jit(solution)/shard_map/jit(_where)/broadcast_in_dim | solution.py:86
  62.1 3.8 %copy.37 = bf16[8,128,1280]{2,1,0:T(8,128)(2,1)S(1)} copy(bf16[8,128,1280]{1,0,2:T(8,128)(2,1)} %all-gather.2.cloned.1.call-done) | data formatting | bytes 5242880 | tf_op jit(solution)/shard_map/all_gather | solution.py:80
  65.9 1.7 %multiply_convert_fusion = bf16[8,128,1280]{2,1,0:T(8,128)(2,1)S(1)} fusion(bf16[8,128,1280]{2,1,0:T(8,128)(2,1)S(1)} %copy.37, f32[8]{0:T(128)S(1)} %compare_convert_fusion, f32[1280]{0:T(1024)S(1)} %get-tuple-element.25, f32[1280]{0:T(1024)S(1)} %get-tuple-element.26), kind=kLoop, calls=%fused_computation | loop fusion | flops 11796480 | bytes 5253152 | tf_op jit(solution)/shard_map/convert_element_type | solution.py:83
  68.1 10.0 %pad_slice_fusion = (bf16[8,128,1280]{2,1,0:T(8,128)(2,1)S(1)}, bf16[8,128,1280]{2,1,0:T(8,128)(2,1)S(1)}, bf16[8,128,1280]{2,1,0:T(8,128)(2,1)S(1)}, bf16[8,128...) fusion(bf16[10,128,1280]{2,1,0:T(8,128)(2,1)S(1)} %maximum_sele, ...), kind=kLoop, calls=%fused_computation.2 | loop fusion | bytes 34734080 | tf_op jit(solution)/shard_map/slice | solution.py:90
  78.1 2.3 %fusion.14 = f32[1024,320]{0,1:T(8,128)S(1)} fusion(bf16[1024,1280]{1,0:T(8,128)(2,1)S(1)} %bitcast.79, bf16[9,1280,320]{1,2,0:T(8,128)(2,1)} %param.12), kind=kOutput, calls=%fused_computation.32 | convolution fusion | flops 838860800 | bytes 4751360 | tf_op jit(solution)/shard_map/dot_general | solution.py:91
  80.5 2.3 %convolution_add_fusion.7 = f32[1024,320]{0,1:T(8,128)S(1)} fusion(f32[1024,320]{0,1:T(8,128)S(1)} %fusion.14, bf16[1024,1280]{1,0:T(8,128)(2,1)S(1)} %bitcast.78, bf16[9,1280,320]{1,2,0:T(8,128)(2,1)} %param.12), kind=kOutput, calls=%fused_computation.20 | convolution fusion | flops 839188480 | bytes 6062080 | tf_op jit(solution)/shard_map/dot_general | solution.py:91
  82.9 1.1 %convolution_add_fusion.6 = f32[1024,320]{0,1:T(8,128)S(1)} fusion(f32[1024,320]{0,1:T(8,128)S(1)} %convolution_add_fusion.7, bf16[1024,1280]{1,0:T(8,128)(2,1)S(1)} %bitcast.77, bf16[9,1280,320]{1,2,0:T(8,128)(2,1)S(1)} %bitcast.81), kind=kOutput, calls=%fused_computation.19 | convolution fusion | flops 839188480 | bytes 6062080 | tf_op jit(solution)/shard_map/dot_general | solution.py:91
  83.9 1.0 %convolution_add_fusion.5 = f32[1024,320]{0,1:T(8,128)S(1)} fusion(f32[1024,320]{0,1:T(8,128)S(1)} %convolution_add_fusion.6, bf16[1024,1280]{1,0:T(8,128)(2,1)S(1)} %bitcast.76, bf16[9,1280,320]{1,2,0:T(8,128)(2,1)S(1)} %bitcast.81), kind=kOutput, calls=%fused_computation.18 | convolution fusion | flops 839188480 | bytes 6062080 | tf_op jit(solution)/shard_map/dot_general | solution.py:91
  85.0 1.1 %convolution_add_fusion.4 = f32[1024,320]{0,1:T(8,128)S(1)} fusion(f32[1024,320]{0,1:T(8,128)S(1)} %convolution_add_fusion.5, bf16[1024,1280]{1,0:T(8,128)(2,1)S(1)} %bitcast.75, bf16[9,1280,320]{1,2,0:T(8,128)(2,1)S(1)} %bitcast.81), kind=kOutput, calls=%fused_computation.17 | convolution fusion | flops 839188480 | bytes 6062080 | tf_op jit(solution)/shard_map/dot_general | solution.py:91
  86.0 1.1 %convolution_add_fusion.3 = f32[1024,320]{0,1:T(8,128)S(1)} fusion(f32[1024,320]{0,1:T(8,128)S(1)} %convolution_add_fusion.4, bf16[1024,1280]{1,0:T(8,128)(2,1)S(1)} %bitcast.74, bf16[9,1280,320]{1,2,0:T(8,128)(2,1)S(1)} %bitcast.81), kind=kOutput, calls=%fused_computation.16 | convolution fusion | flops 839188480 | bytes 6062080 | tf_op jit(solution)/shard_map/dot_general | solution.py:91
  87.1 1.1 %convolution_add_fusion.2 = f32[1024,320]{0,1:T(8,128)S(1)} fusion(f32[1024,320]{0,1:T(8,128)S(1)} %convolution_add_fusion.3, bf16[1024,1280]{1,0:T(8,128)(2,1)S(1)} %bitcast.73, bf16[9,1280,320]{1,2,0:T(8,128)(2,1)S(1)} %bitcast.81), kind=kOutput, calls=%fused_computation.15 | convolution fusion | flops 839188480 | bytes 6062080 | tf_op jit(solution)/shard_map/dot_general | solution.py:91
  88.2 1.1 %convolution_add_fusion.1 = f32[1024,320]{0,1:T(8,128)S(1)} fusion(f32[1024,320]{0,1:T(8,128)S(1)} %convolution_add_fusion.2, bf16[1024,1280]{1,0:T(8,128)(2,1)S(1)} %bitcast.72, bf16[9,1280,320]{1,2,0:T(8,128)(2,1)S(1)} %bitcast.81), kind=kOutput, calls=%fused_computation.14 | convolution fusion | flops 839188480 | bytes 6062080 | tf_op jit(solution)/shard_map/dot_general | solution.py:91
  89.2 1.1 %fusion.2 = f32[40,8,8,128]{3,2,1,0:T(8,128)S(1)} fusion(f32[1024,320]{0,1:T(8,128)S(1)} %convolution_add_fusion.1, bf16[1024,1280]{1,0:T(8,128)(2,1)S(1)} %bitcast.71, bf16[9,1280,320]{1,2,0:T(8,128)(2,1)S(1)} %bitcast.81), kind=kOutput, calls=%fused_computation.13 | convolution fusion | flops 839188480 | bytes 6062080 | tf_op jit(solution)/shard_map/dot_general | solution.py:91
  90.8 1.9 %copy.39 = bf16[16,128,320]{2,0,1:T(8,128)(2,1)} copy(bf16[16,128,320]{1,2,0:T(8,128)(2,1)S(1)} %bitcast.70) | data formatting | bytes 2621440 | tf_op jit(solution)/shard_map/reshape | solution.py:95
  92.6 1.7 %broadcast_in_dim.42 = bf16[16,128,2,320]{3,0,2,1:T(8,128)(2,1)S(1)} broadcast(bf16[16,128,320]{2,0,1:T(8,128)(2,1)} %copy.39), dimensions={0,1,3} | broadcast | bytes 3932160 | tf_op jit(solution)/shard_map/broadcast_in_dim | solution.py:95
  94.3 3.1 %copy.40 = bf16[16,256,320]{1,2,0:T(8,128)(2,1)} copy(bf16[16,256,320]{2,0,1:T(8,128)(2,1)S(1)} %bitcast.69) | data formatting | bytes 5242880
  (52 shorter events, 3.7 us)
Async XLA Ops:
  7.2 10.6 %copy-start = (bf16[8,128,320]{1,2,0:T(8,128)(2,1)S(1)}, bf16[8,128,320]{1,2,0:T(8,128)(2,1)}, u32[]{:S(2)}) copy-start(bf16[8,128,320]{1,2,0:T(8,128)(2,1)} %param.11) | copy-start | bytes 1966084
  7.2 11.0 %copy-start.3 = (s32[1280]{0:T(1024)S(1)}, s32[1280]{0:T(1024)}, u32[]{:S(2)}) copy-start(s32[1280]{0:T(1024)} %param.15) | copy-start | bytes 15364
  7.2 18.3 %copy-start.6 = (f32[1,32]{1,0:T(1,128)S(1)}, f32[1,32]{1,0:T(1,128)}, u32[]{:S(2)}) copy-start(f32[1,32]{1,0:T(1,128)} %param.21) | copy-start | bytes 388
  7.2 18.3 %copy-start.8 = (f32[1,32]{1,0:T(1,128)S(1)}, f32[1,32]{1,0:T(1,128)}, u32[]{:S(2)}) copy-start(f32[1,32]{1,0:T(1,128)} %param.20) | copy-start | bytes 388
  7.2 18.3 %copy-start.7 = (f32[32]{0:T(128)S(1)}, f32[32]{0:T(128)}, u32[]{:S(2)}) copy-start(f32[32]{0:T(128)} %param.19) | copy-start | bytes 388
  7.2 18.3 %copy-start.9 = (f32[32]{0:T(128)S(1)}, f32[32]{0:T(128)}, u32[]{:S(2)}) copy-start(f32[32]{0:T(128)} %param.18) | copy-start | bytes 388
  7.2 41.2 %copy-start.4 = (f32[1280]{0:T(1024)S(1)}, f32[1280]{0:T(1024)}, u32[]{:S(2)}) copy-start(f32[1280]{0:T(1024)} %param.14) | copy-start | bytes 15364
  7.2 41.2 %copy-start.5 = (f32[1280]{0:T(1024)S(1)}, f32[1280]{0:T(1024)}, u32[]{:S(2)}) copy-start(f32[1280]{0:T(1024)} %param.13) | copy-start | bytes 15364
  7.2 54.8 %all-gather.2.cloned.1.call-start = ((), (), s32[]{:S(2)}) async-start(), calls=%async_computation | async-start | bytes 3276800 | tf_op jit(solution)/shard_map/all_gather | solution.py:80
  10.8 14.6 %collective-permute-start = (bf16[1,128,320]{2,1,0:T(8,128)(2,1)S(1)}, bf16[1,128,320]{2,1,0:T(8,128)(2,1)S(1)}, u32[]{:S(2)}, u32[]{:S(2)}) collective-permute-start(bf16[1,128,320]{2,1,0:T(8,128)(2,1)S(1)} %copy.41), channel_id=1, source_target_pairs={{0,4},{4,8},{8,12},{12,16},{16,20},{20,24},{24,28},{1,5},{5,9},{9,... | collective-permute-start | bytes 245768 | tf_op jit(solution)/shard_map/ppermute | solution.py:25
  15.8 9.5 %collective-permute-start.1 = (bf16[1,128,320]{2,1,0:T(8,128)(2,1)S(1)}, bf16[1,128,320]{2,1,0:T(8,128)(2,1)S(1)}, u32[]{:S(2)}, u32[]{:S(2)}) collective-permute-start(bf16[1,128,320]{2,1,0:T(8,128)(2,1)S(1)} %copy.42), channel_id=1, source_target_pairs={{4,0},{8,4},{12,8},{16,12},{20,16},{24,20},{28,24},{5,1},{9,5},{13... | collective-permute-start | bytes 245768 | tf_op jit(solution)/shard_map/ppermute | solution.py:28
  25.4 22.9 %collective-permute-start.2 = (bf16[2,128,320]{2,1,0:T(8,128)(2,1)S(1)}, bf16[2,128,320]{2,1,0:T(8,128)(2,1)S(1)}, u32[]{:S(2)}, u32[]{:S(2)}) collective-permute-start(bf16[2,128,320]{2,1,0:T(8,128)(2,1)S(1)} %constant_dynamic-update-slice_fusion), channel_id=1, source_target_pairs={{0,1},{1,2},{2,3},{3,0},{4,5},{5,6},{6,7},{7,4},{8,9},{9,10},{10,1... | collective-permute-start | bytes 491528 | tf_op jit(solution)/shard_map/ppermute | solution.py:14
  48.3 5.1 %collective-permute-start.3 = (bf16[2,128,320]{2,1,0:T(8,128)(2,1)S(1)}, bf16[2,128,320]{2,1,0:T(8,128)(2,1)S(1)}, u32[]{:S(2)}, u32[]{:S(2)}) collective-permute-start(bf16[2,128,320]{2,1,0:T(8,128)(2,1)S(1)} %collective-permute-done.2), channel_id=1, source_target_pairs={{0,1},{1,2},{2,3},{3,0},{4,5},{5,6},{6,7},{7,4},{8,9},{9,10},{10,1... | collective-permute-start | bytes 491528 | tf_op jit(solution)/shard_map/ppermute | solution.py:14
  53.5 5.1 %collective-permute-start.4 = (bf16[2,128,320]{2,1,0:T(8,128)(2,1)S(1)}, bf16[2,128,320]{2,1,0:T(8,128)(2,1)S(1)}, u32[]{:S(2)}, u32[]{:S(2)}) collective-permute-start(bf16[2,128,320]{2,1,0:T(8,128)(2,1)S(1)} %collective-permute-done.3), channel_id=1, source_target_pairs={{0,1},{1,2},{2,3},{3,0},{4,5},{5,6},{6,7},{7,4},{8,9},{9,10},{10,1... | collective-permute-start | bytes 491528 | tf_op jit(solution)/shard_map/ppermute | solution.py:14
  65.9 1.7 %copy-start.1 = (bf16[128,1280]{1,0:T(8,128)(2,1)S(1)}, bf16[128,1280]{1,0:T(8,128)(2,1)}, u32[]{:S(2)}) copy-start(bf16[128,1280]{1,0:T(8,128)(2,1)} %get-tuple-element.38) | copy-start | bytes 983044
  65.9 1.7 %copy-start.2 = (bf16[1,128,1280]{2,1,0:T(8,128)(2,1)S(1)}, bf16[1,128,1280]{2,1,0:T(8,128)(2,1)}, u32[]{:S(2)}) copy-start(bf16[1,128,1280]{2,1,0:T(8,128)(2,1)} %get-tuple-element.39) | copy-start | bytes 983044
  78.1 4.7 %slice-start = ((s8[7372800]{0:T(1024)(128)(4,1)}), s8[4194304]{0:T(1024)(128)(4,1)S(1)}, s32[]{:S(2)}) async-start(s8[7372800]{0:T(1024)(128)(4,1)} %bitcast.80), calls=%async_computation.1 | async-start | bytes 8388608
  80.5 2.4 %slice-start.1 = ((s8[7372800]{0:T(1024)(128)(4,1)}), s8[3178496]{0:T(1024)(128)(4,1)S(1)}, s32[]{:S(2)}) async-start(s8[7372800]{0:T(1024)(128)(4,1)} %bitcast.80), calls=%async_computation.2 | async-start | bytes 6356992
Sparse Core Ops, SparseCore 0:
  10.2 30.4 all-gather.1
